TPU v7x, 32 devices: a whole 2x2x4 slice. The times are simulated.
32 devices in a mesh: ma: 8 (over z, y), vert: 4 (over x, core).
Axes of the slice: x: 2, y: 2, z: 4, core: 2. Of those that a mesh axis runs over, the one named last changes fastest.
Arguments:
- trial_block: bfloat16 [128, 64, 4, 1024], P('vert', 'ma'), may hold values from -6 to 6
- legendre: bfloat16 [64, 2, 32, 1024], P('ma'), may hold values from -0.1875 to 0.1875
- order_slot: int32 [64], replicated, may hold values from 0 to 63, each once
- cycle_start: int32 [32], replicated, may hold values from 0 to 127
- cycle_count: int32 [32], replicated, may hold values from 0 to 128, as said below
- cycle_weight: float32 [32], replicated, may hold values from 4 to 32
Outputs:
- new_basis: bfloat16 [128, 64, 4, 1024], P('vert', 'ma')
- ritz_matrix: float32 [128, 128], replicated
Inputs may be any that keep to these rules, and one draw needn't show every extreme that they name: `cycle_count`: exactly 8 consecutive cycles have a nonzero count, and one of them has 128.
All inputs are finite; a program needn't handle non-finite values.
Results may differ from a plain program's by a relative error of at most 0.0073.
The roundings to bfloat16 on the way count: a program that leaves them out, or rounds other values in their place, can miss the bound.
Values may be sent and summed in bfloat16 or wider, within the bound.
A program may use at most 192 MiB of HBM per device.

v0:
```python
import functools
import math

import jax
import jax.numpy as jnp
from jax import lax
from jax.experimental import pallas as pl
from jax.experimental.pallas import tpu as pltpu
from jax.sharding import PartitionSpec as P

MESH = pl.DeviceIdType.MESH
VMEM = pltpu.VMEM
SMEM = pltpu.SMEM
DMA = pltpu.SemaphoreType.DMA
F32 = jnp.float32
BF16 = jnp.bfloat16
I32 = jnp.int32
HIGHEST = lax.Precision.HIGHEST
GRANT = 60 * 1024 * 1024
LANES = 128
PANEL = 16
NT = (((1,), (1,)), ((), ()))
STAGES = (7, 12)


def iota(shape, axis):
    return lax.broadcasted_iota(I32, shape, axis)


def mm(a, b):
    return jnp.dot(a, b, preferred_element_type=F32)


def mm_nt(a, b):
    return lax.dot_general(a, b, NT, preferred_element_type=F32)


def split(x, count):
    pieces = []
    for _ in range(count):
        piece = x.astype(BF16)
        pieces.append(piece)
        x = x - piece.astype(F32)
    return pieces


def swap(x):
    return pltpu.roll(x, x.shape[1] // 2, 1)


def half_sign(shape, first, second):
    return jnp.where(iota(shape, 1) < shape[1] // 2, first, second).astype(F32)


def rows_at(index, count):
    return pl.ds(pl.multiple_of(index * count, count), count)


def factor_panel(work, p):
    size = work.shape[0]
    first = pl.multiple_of(p * PANEL, PANEL)
    at = pl.ds(first, PANEL)
    lane = iota((PANEL, size), 1)
    sub = iota((PANEL, 2 * size), 0)
    x = work[at, :]
    column = [
        jnp.sum(jnp.where(lane == first + i, x[:, :size], 0.0), axis=1, keepdims=True)
        for i in range(PANEL)
    ]
    for i in range(PANEL):
        inverse = lax.rsqrt(column[i][i : i + 1, :])
        scaled = column[i] * inverse
        for k in range(i + 1, PANEL):
            column[k] = column[k] - scaled * (column[k][i : i + 1, :] * inverse)
        line = x[i : i + 1, :] * inverse
        x = jnp.where(sub == i, line, jnp.where(sub > i, x - scaled * line, x))
    update = lax.dot_general(
        x[:, :size], x, (((0,), (0,)), ((), ())),
        precision=HIGHEST, preferred_element_type=F32,
    )
    below = iota((size, 2 * size), 0) >= first + PANEL
    work[...] = jnp.where(below, work[...] - update, work[...])
    work[at, :] = x


def cosines(phase, total):
    phase = jnp.where(phase > total // 2, total - phase, phase)
    turned = phase > total // 4
    x = jnp.where(turned, total // 2 - phase, phase).astype(F32) * (2.0 * math.pi / total)
    y = x * x
    value = jnp.full_like(y, 1.0 / math.factorial(12))
    for n in (10, 8, 6, 4, 2, 0):
        value = value * y * (1.0 if n % 4 == 2 else 1.0) + (-1.0) ** (n // 2) / math.factorial(n)
    return jnp.where(turned, -value, value)


def modulo(x, total):
    return x & (total - 1) if total & (total - 1) == 0 else lax.rem(x, total)


def step_kernel(
    n_ma, n_vert, live,
    trial_ref, legendre_ref, order_ref, start_ref, count_ref, weight_ref,
    rows_ref, ab_ref, mixer_ref, leg_ref,
    native, leg_in, near, far, message, gathered, spectra, returned, packed,
    row_a, land_a, sum_a, row_b, land_b, ab_own, land_c, ab_mid, land_d,
    work, lhs, llm, tables, back_table,
    load_sem, leg_sem, near_send, near_recv, far_send, far_recv,
    ma_send, ma_recv, vert_send, vert_recv,
):
    ma = lax.axis_index("ma")
    vert = lax.axis_index("vert")
    pairs, vectors, _, per, _ = native.shape
    orders = 2 * pairs
    parts, degrees = near.shape[2], near.shape[4]
    tiles = degrees // LANES
    cycles = leg_in.shape[2]
    half = n_vert // 2
    share = orders // n_vert
    place = lax.rem(vert, half)
    side = vert // half
    total = n_vert * vectors
    terms = live * orders
    longitudes = 2 * n_ma * orders

    barrier = pltpu.get_barrier_semaphore()

    def ma_peer(step):
        return lax.rem(ma + step, n_ma)

    def vert_peer(step):
        return lax.rem(vert + step, n_vert)

    def greet_ma(step, carry):
        pl.semaphore_signal(barrier, inc=1, device_id=(ma_peer(step), vert), device_id_type=MESH)
        return carry

    def greet_vert(step, carry):
        pl.semaphore_signal(barrier, inc=1, device_id=(ma, vert_peer(step)), device_id_type=MESH)
        return carry

    lax.fori_loop(1, n_ma, greet_ma, 0)
    lax.fori_loop(1, n_vert, greet_vert, 0)

    def load(pair):
        at = pl.ds(2 * pair, 2)
        return pltpu.make_async_copy(trial_ref.at[:, at], native.at[pair], load_sem.at[pair])

    def pair_at(i):
        return lax.rem((1 - side) * (orders // 4) + i, orders // 2)

    for i in range(orders // 2):
        load(pair_at(i)).start()
    leg_copy = pltpu.make_async_copy(legendre_ref, leg_in, leg_sem)
    leg_copy.start()

    rows = 8 * per
    row = iota((rows, rows), 0)
    column = iota((rows, rows), 1)
    wanted = lax.rem(row, 8) * per + lax.rem(row // 8, tiles) * parts + row // (8 * tiles)
    reorder = (column == wanted).astype(BF16)

    for i in range(orders // 2):
        load(pair_at(i)).wait()
    leg_copy.wait()

    def arrange(i, carry):
        pair = pair_at(i)
        for g in range(vectors // 16):
            blocks = []
            for h in range(2):
                at = pl.ds(16 * g + 8 * h, 8)
                both = [native[pair, at, e].reshape(rows, LANES) for e in range(2)]
                blocks.append(mm(reorder, jnp.concatenate(both, axis=1)))
            for e in range(2):
                for c in range(parts):
                    for t in range(tiles):
                        lo = (c * tiles + t) * 8
                        at = (slice(lo, lo + 8), slice(e * LANES, (e + 1) * LANES))
                        tile = jnp.concatenate([blocks[0][at], blocks[1][at]], axis=0)
                        at = (slice(16 * g, 16 * g + 16), slice(t * LANES, (t + 1) * LANES))
                        near[(place, 2 * pair + e, c) + at] = tile.astype(BF16)
        return carry

    lax.fori_loop(0, orders // 2, arrange, 0)

    def search(i, found):
        j = cycles - 1 - i
        return jnp.where(count_ref[j] > 0, j, found)

    first = jnp.minimum(lax.fori_loop(0, cycles, search, 0), cycles - live)

    block = min(terms, 64)
    for kind in range(2):
        source = leg_in[:, kind].reshape(orders * cycles, degrees)

        def pick(i, carry):
            row = iota((block, orders * cycles), 0) + i * block
            column = iota((block, orders * cycles), 1)
            wanted = lax.rem(row, orders) * cycles + row // orders + first
            at = rows_at(kind * (terms // block) + i, block)
            leg_ref[at, :] = mm((column == wanted).astype(BF16), source).astype(BF16)
            return carry

        lax.fori_loop(0, terms // block, pick, 0)

    pl.semaphore_wait(barrier, n_ma + n_vert - 2)

    def near_copy(peer, slot, source):
        return pltpu.make_async_remote_copy(
            src_ref=near.at[source],
            dst_ref=near.at[source],
            send_sem=near_send.at[slot],
            recv_sem=near_recv.at[slot],
            device_id=(ma, peer),
            device_id_type=MESH,
        )

    pieces = half * share * parts

    def far_copy(piece, arriving=False):
        offset = lax.rem(piece, half)
        inner = piece // half
        peer = (1 - side) * half + lax.rem(place + offset, half)
        slot = lax.rem(place + half - offset, half) if arriving else place
        s = inner // parts
        c = lax.rem(inner, parts)
        return pltpu.make_async_remote_copy(
            src_ref=near.at[slot, peer * share + s, c],
            dst_ref=far.at[slot, s, c],
            send_sem=far_send.at[piece],
            recv_sem=far_recv.at[piece],
            device_id=(ma, peer),
            device_id_type=MESH,
        )

    def send_far(begin, end):
        def body(piece, carry):
            far_copy(piece).start()
            return carry

        lax.fori_loop(begin, end, body, 0)

    cuts = [min(pieces, cut) for cut in STAGES]
    send_far(0, cuts[0])
    for step in range(1, half):
        near_copy(side * half + lax.rem(place + step, half), step, place).start()

    keep = lax.rem(iota((2 * terms, LANES), 0), orders)

    def product(s, carry):
        vectors_here = near[place, s].reshape(parts * vectors, degrees)
        found = mm_nt(leg_ref[...], vectors_here)
        spectra[...] = jnp.where(keep == s, found, spectra[...])
        return carry

    lax.fori_loop(0, orders, product, 0)
    w = spectra[:terms, :]
    x = spectra[terms:, :]
    quarter = iota((terms, LANES), 1) // vectors
    left = lambda a: pltpu.roll(a, LANES - vectors, 1)
    right = lambda a: pltpu.roll(a, vectors, 1)
    w = jnp.where(quarter == 1, left(w), jnp.where(quarter == 2, right(w), w))
    x = jnp.where(quarter == 0, right(x), jnp.where(quarter == 3, left(x), x))
    w = jnp.where((quarter == 1) | (quarter == 3), -w, w)
    fields = w + jnp.where(quarter >= 2, -x, x)
    front = iota((orders, LANES), 1) < LANES // 2
    for pair in range(live // 2):
        a = fields[2 * pair * orders : (2 * pair + 1) * orders]
        b = fields[(2 * pair + 1) * orders : (2 * pair + 2) * orders]
        both = jnp.concatenate([jnp.where(front, a, swap(b)), jnp.where(front, swap(a), b)], axis=0)
        message[:, pair * LANES : (pair + 1) * LANES] = both.astype(BF16)

    def ma_copy(kind, source, target, slot, peer):
        return pltpu.make_async_remote_copy(
            src_ref=source,
            dst_ref=target.at[slot],
            send_sem=ma_send.at[kind, peer],
            recv_sem=ma_recv.at[kind, slot],
            device_id=(peer, vert),
            device_id_type=MESH,
        )

    def over_ma(act):
        def body(step, carry):
            act(ma_peer(step))
            return carry

        lax.fori_loop(1, n_ma, body, 0)

    def ma_start(kind, source, target):
        over_ma(lambda peer: ma_copy(kind, source, target, ma, peer).start())

    def ma_wait(kind, source, target):
        over_ma(lambda peer: ma_copy(kind, source, target, peer, peer).wait_recv())

    def ma_done(kind, source, target):
        over_ma(lambda peer: ma_copy(kind, source, target, ma, peer).wait_send())

    def vert_copy(kind, source, target, slot, peer):
        return pltpu.make_async_remote_copy(
            src_ref=source,
            dst_ref=target.at[slot],
            send_sem=vert_send.at[kind, peer],
            recv_sem=vert_recv.at[kind, slot],
            device_id=(ma, peer),
            device_id_type=MESH,
        )

    def over_vert(act):
        def body(step, carry):
            act(vert_peer(step))
            return carry

        lax.fori_loop(1, n_vert, body, 0)

    def vert_start(kind, source, target):
        over_vert(lambda peer: vert_copy(kind, source, target, vert, peer).start())

    def vert_wait(kind, source, target):
        over_vert(lambda peer: vert_copy(kind, source, target, peer, peer).wait_recv())

    def vert_done(kind, source, target):
        over_vert(lambda peer: vert_copy(kind, source, target, vert, peer).wait_send())

    ma_start(0, message, gathered)
    gathered[ma] = message[...]

    turned = spectra[...].T
    part = [turned[c * vectors : (c + 1) * vectors] for c in range(parts)]
    wide = part[0].shape
    sign = half_sign(wide, 1.0, -1.0)
    field_x = (part[0] + swap(part[3])) * sign
    field_y = part[1] - swap(part[2])
    for n, (piece_x, piece_y) in enumerate(zip(split(field_x, 3), split(field_y, 3))):
        at = slice((3 + n) * vectors, (4 + n) * vectors)
        lhs[at, : 2 * terms] = piece_x
        lhs[at, 2 * terms :] = piece_y

    step_rows = min(2 * terms, LANES)

    def leg_products(i, carry):
        at = rows_at(i, step_rows)
        found = mm_nt(leg_ref[at, :], leg_ref[...])
        same = lax.rem(iota(found.shape, 0) - iota(found.shape, 1) + 2 * terms * orders, orders) == 0
        for n, piece in enumerate(split(jnp.where(same, found, 0.0), 3)):
            llm[n, at, :] = piece
        return carry

    lax.fori_loop(0, 2 * terms // step_rows, leg_products, 0)

    scale = 1.0 / math.sqrt(n_ma * orders)
    width = n_ma * 2 * orders
    lane = iota((8, width), 1)
    slot = lane // (2 * orders) * orders + lax.rem(lane, orders)

    def place_order(i, carry):
        return jnp.where(slot == i, order_ref[i], carry)

    lane_order = lax.fori_loop(0, n_ma * orders, place_order, jnp.zeros((8, width), I32))
    shift = jnp.where(lax.rem(lane // orders, 2) == 1, longitudes - longitudes // 4, 0)

    def table_rows(i, carry):
        j = iota((LANES, width), 0) + i * LANES
        phase = modulo(j * lane_order[:1] + shift[:1], longitudes)
        tables[rows_at(i, LANES), :] = (cosines(phase, longitudes) * scale).astype(BF16)
        return carry

    lax.fori_loop(0, longitudes // LANES, table_rows, 0)
    row = iota((2 * orders, longitudes), 0)
    own_order = jnp.zeros((2 * orders, longitudes), I32)
    for s in range(orders):
        own_order = jnp.where(lax.rem(row, orders) == s, order_ref[ma * orders + s], own_order)
    phase = iota((2 * orders, longitudes), 1) * own_order
    phase = phase + jnp.where(row >= orders, longitudes - longitudes // 4, 0)
    back_table[...] = (cosines(modulo(phase, longitudes), longitudes) * scale).astype(BF16)

    for step in range(1, half):
        peer = side * half + lax.rem(place + step, half)
        near_copy(peer, half - step, lax.rem(place + step, half)).wait_recv()

    def near_gram(s, sums):
        for c in range(parts):
            sums = sums + mm_nt(near[place, s, c], near[:, s, c].reshape(half * vectors, degrees))
        return sums

    near_sums = lax.fori_loop(0, orders, near_gram, jnp.zeros((vectors, half * vectors), F32))
    row_b[:, total:] = jnp.concatenate([near_sums, jnp.zeros_like(near_sums)], axis=1)

    ma_wait(0, message, gathered)
    columns = message.shape[1]
    wide_block = min(columns, 512)
    cycles_here = wide_block // (2 * vectors)

    def transform(block, carry):
        at = rows_at(block, wide_block)
        grid = mm(tables[...], gathered[:, :, at].reshape(n_ma * 2 * orders, wide_block))
        lane_cycle = iota((8, wide_block), 1) // (2 * vectors)
        begin = jnp.zeros((8, wide_block), I32)
        length = jnp.zeros((8, wide_block), I32)
        weight = jnp.zeros((8, wide_block), F32)
        for r in range(cycles_here):
            here = lane_cycle == r
            cycle = first + block * cycles_here + r
            begin = jnp.where(here, start_ref[cycle], begin)
            length = jnp.where(here, count_ref[cycle], length)
            weight = jnp.where(here, weight_ref[cycle], weight)
        away = iota(grid.shape, 0) - begin[:1]
        away = jnp.where(away < 0, away + longitudes, away)
        weighted = (grid * jnp.where(away < length[:1], weight[:1], 0.0)).astype(BF16)
        found = mm(back_table[...], weighted)
        for n in range(wide_block // LANES):
            both = found[:, n * LANES : (n + 1) * LANES]
            c, s = both[:orders], both[orders:]
            pair = [jnp.where(front, c, swap(s)), jnp.where(front, swap(c), s)]
            for e in range(2):
                cycle = block * cycles_here + 2 * n + e
                returned[rows_at(cycle, orders), :] = pair[e]
        return carry

    lax.fori_loop(0, columns // wide_block, transform, 0)
    here = returned[...]
    even = lax.rem(iota(here.shape, 1) // vectors, 2) == 0
    turned = jnp.concatenate([here, jnp.where(even, right(here), left(here))], axis=0).T
    turned = turned.astype(BF16)
    g_x = turned[:vectors]
    back_y = turned[vectors : 2 * vectors]
    g_y = turned[2 * vectors : 3 * vectors]
    back_x = turned[3 * vectors :]
    packed[vert, :, : 2 * terms] = g_x
    packed[vert, :, 2 * terms :] = g_y
    vert_start(0, packed.at[vert], packed)
    send_far(cuts[0], cuts[1])

    signs = sign.astype(BF16)
    adjoint = jnp.concatenate([g_x * signs, g_y, -back_y, -back_x * signs], axis=0)
    products = mm(adjoint, llm[0]) + mm(adjoint, llm[1]) + mm(adjoint, llm[2])
    part = [products[c * vectors : (c + 1) * vectors] for c in range(parts)]
    gram_x = part[0] * sign + swap(part[3] * -sign)
    gram_y = part[1] - swap(part[2])
    for n, (piece_x, piece_y) in enumerate(zip(split(gram_x, 3), split(gram_y, 3))):
        at = slice(n * vectors, (n + 1) * vectors)
        lhs[at, : 2 * terms] = piece_x
        lhs[at, 2 * terms :] = piece_y

    vert_wait(0, packed.at[vert], packed)
    everyone = packed[...].reshape(total, 4 * terms)
    found = mm_nt(lhs[...], everyone)
    found = [found[n * vectors : (n + 1) * vectors] for n in range(6)]
    row_a[...] = found[0] + found[1] + found[2]
    ma_start(1, row_a, land_a)
    land_a[ma] = row_a[...]
    row_b[:, :total] = found[3] + found[4] + found[5]
    ma_start(2, row_b, land_b)
    land_b[ma] = row_b[...]
    ma_wait(1, row_a, land_a)
    sum_a[vert] = jnp.sum(land_a[...], axis=0)
    vert_start(1, sum_a.at[vert], sum_a)
    ma_wait(2, row_b, land_b)
    rows_ref[vert] = jnp.sum(land_b[...], axis=0)
    vert_start(2, rows_ref.at[vert], rows_ref)
    send_far(cuts[1], pieces)

    vert_wait(1, sum_a.at[vert], sum_a)
    inverse_count = 1.0 / (n_ma * orders * parts * degrees)
    work[:, :total] = sum_a[...].reshape(total, total) * inverse_count
    work[:, total:] = (iota((total, total), 0) == iota((total, total), 1)).astype(F32)

    def panel_step(p, carry):
        factor_panel(work, p)
        return carry

    panels = total // PANEL
    lax.fori_loop(0, panels // 2, panel_step, 0)

    def far_wait(piece, carry):
        far_copy(piece, True).wait_recv()
        return carry

    lax.fori_loop(0, pieces, far_wait, 0)

    def far_gram(s, sums):
        for c in range(parts):
            here = near[:, vert * share + s, c].reshape(half * vectors, degrees)
            sums = sums + mm_nt(here, far[:, s, c].reshape(half * vectors, degrees))
        return sums

    cross_sums = lax.fori_loop(
        0, share, far_gram, jnp.zeros((half * vectors, half * vectors), F32)
    )
    cross_sums = jnp.where(side == 0, cross_sums, cross_sums.T)
    size = half * vectors
    ab_own[...] = jnp.concatenate([cross_sums[: size // 2], cross_sums[size // 2 :]], axis=1)
    vert_start(3, ab_own, land_c)
    land_c[vert] = ab_own[...]
    lax.fori_loop(panels // 2, panels, panel_step, 0)
    vert_wait(3, ab_own, land_c)
    ab_mid[...] = jnp.sum(land_c[...], axis=0)
    ma_start(3, ab_mid, land_d)
    land_d[ma] = ab_mid[...]

    mixing = work[rows_at(vert, vectors), total:].astype(BF16)
    spread = (iota((parts * vectors, vectors), 0) // parts == iota((parts * vectors, vectors), 1))
    mixing = mm(spread.astype(BF16), mixing).astype(BF16)
    mixed = mm(mixing, everyone)
    mixed_x, mixed_y = mixed[:, : 2 * terms], mixed[:, 2 * terms :]
    kind = lax.rem(iota(mixed_x.shape, 0), parts)
    sign = half_sign(mixed_x.shape, 1.0, -1.0)
    mixer = jnp.where(
        kind == 0, mixed_x * sign,
        jnp.where(kind == 1, mixed_y, jnp.where(kind == 2, -swap(mixed_y), -swap(mixed_x) * sign)),
    )
    high, low = split(mixer, 2)
    mixer_ref[:, : 2 * terms] = high
    mixer_ref[:, 2 * terms :] = low

    vert_wait(2, rows_ref.at[vert], rows_ref)
    ma_wait(3, ab_mid, land_d)
    ab_ref[...] = jnp.sum(land_d[...], axis=0)

    for step in range(1, half):
        near_copy(side * half + lax.rem(place + step, half), step, place).wait_send()

    def far_done(piece, carry):
        far_copy(piece).wait_send()
        return carry

    lax.fori_loop(0, pieces, far_done, 0)
    ma_done(0, message, gathered)
    vert_done(0, packed.at[vert], packed)
    ma_done(1, row_a, land_a)
    ma_done(2, row_b, land_b)
    vert_done(1, sum_a.at[vert], sum_a)
    vert_done(2, rows_ref.at[vert], rows_ref)
    vert_done(3, ab_own, land_c)
    ma_done(3, ab_mid, land_d)


def step_terms(trial, legendre, order_slot, cycle_start, cycle_count, cycle_weight, n_ma, n_vert):
    vectors, orders, per, _ = trial.shape
    _, kinds, cycles, degrees = legendre.shape
    parts = per * LANES // degrees
    live = cycles // 4
    terms = live * orders
    total = n_vert * vectors
    half = n_vert // 2
    share = orders // n_vert
    longitudes = 2 * n_ma * orders
    pieces = half * share * parts
    columns = live * 2 * vectors
    anywhere = pl.BlockSpec(memory_space=pl.ANY)
    return pl.pallas_call(
        functools.partial(step_kernel, n_ma, n_vert, live),
        out_shape=(
            jax.ShapeDtypeStruct((n_vert, vectors, total + 2 * half * vectors), F32),
            jax.ShapeDtypeStruct((half * vectors // 2, 2 * half * vectors), F32),
            jax.ShapeDtypeStruct((parts * vectors, 4 * terms), BF16),
            jax.ShapeDtypeStruct((2 * terms, degrees), BF16),
        ),
        in_specs=[anywhere, anywhere] + [pl.BlockSpec(memory_space=SMEM)] * 4,
        out_specs=[pl.BlockSpec(memory_space=VMEM)] * 4,
        scratch_shapes=[
            VMEM((orders // 2, vectors, 2, per, LANES), BF16),
            VMEM(legendre.shape, BF16),
            VMEM((half, orders, parts, vectors, degrees), BF16),
            VMEM((half, share, parts, vectors, degrees), BF16),
            VMEM((2 * orders, columns), BF16),
            VMEM((n_ma, 2 * orders, columns), BF16),
            VMEM((2 * terms, LANES), F32),
            VMEM((terms, LANES), F32),
            VMEM((n_vert, vectors, 4 * terms), BF16),
            VMEM((vectors, total), F32),
            VMEM((n_ma, vectors, total), F32),
            VMEM((n_vert, vectors, total), F32),
            VMEM((vectors, total + 2 * half * vectors), F32),
            VMEM((n_ma, vectors, total + 2 * half * vectors), F32),
            VMEM((half * vectors // 2, 2 * half * vectors), F32),
            VMEM((n_vert, half * vectors // 2, 2 * half * vectors), F32),
            VMEM((half * vectors // 2, 2 * half * vectors), F32),
            VMEM((n_ma, half * vectors // 2, 2 * half * vectors), F32),
            VMEM((total, 2 * total), F32),
            VMEM((6 * vectors, 4 * terms), BF16),
            VMEM((3, 2 * terms, 2 * terms), BF16),
            VMEM((longitudes, n_ma * 2 * orders), BF16),
            VMEM((2 * orders, longitudes), BF16),
            DMA((orders // 2,)),
            DMA,
            DMA((half,)),
            DMA((half,)),
            DMA((pieces,)),
            DMA((pieces,)),
            DMA((4, n_ma)),
            DMA((4, n_ma)),
            DMA((4, n_vert)),
            DMA((4, n_vert)),
        ],
        compiler_params=pltpu.CompilerParams(
            collective_id=0, has_side_effects=True, vmem_limit_bytes=GRANT
        ),
        name="step_terms",
    )(trial, legendre, order_slot, cycle_start, cycle_count, cycle_weight)


def finish_kernel(
    coefficients, rows_ref, ab_ref, mixer_ref, leg_ref, basis_ref, ritz_ref, work, staged, sems
):
    total = ritz_ref.shape[0]
    size = total // 2
    orders, vectors, parts, degrees = staged.shape
    scale = 1.0 / coefficients
    own = rows_ref[...].reshape(total, rows_ref.shape[2])
    ab = ab_ref[...]
    ab = jnp.concatenate([ab[:, :size], ab[:, size:]], axis=0)
    top = jnp.concatenate([own[:size, total : total + size], ab], axis=1)
    bottom = jnp.concatenate([ab.T, own[size:, total : total + size]], axis=1)
    work[:, :total] = jnp.concatenate([top, bottom], axis=0) * scale
    work[:, total:] = (iota((total, total), 0) == iota((total, total), 1)).astype(F32)
    mixer = mixer_ref[...]
    lane_order = lax.rem(iota(mixer.shape, 1), orders)

    def out_copy(s):
        return pltpu.make_async_copy(staged.at[s], basis_ref.at[:, s], sems.at[s])

    def mix(s):
        picked = jnp.where(lane_order == s, mixer, jnp.zeros_like(mixer))
        width = mixer.shape[1] // 2
        mixed = mm(picked[:, :width], leg_ref[...]) + mm(picked[:, width:], leg_ref[...])
        staged[s] = mixed.reshape(vectors, parts, degrees).astype(BF16)
        out_copy(s).start()

    panels = total // PANEL
    assert panels == orders

    def step(p, carry):
        factor_panel(work, p)
        mix(p)
        return carry

    lax.fori_loop(0, panels, step, 0)
    inverse = work[:, total:]
    half = jnp.dot(inverse, own[:, :total] * scale, precision=HIGHEST, preferred_element_type=F32)
    ritz_ref[...] = lax.dot_general(
        half, inverse, NT, precision=HIGHEST, preferred_element_type=F32
    )

    def done(s, carry):
        out_copy(s).wait()
        return carry

    lax.fori_loop(0, orders, done, 0)


def finish(rows, ab, mixer, table, vectors, orders, coefficients):
    total = rows.shape[0] * rows.shape[1]
    degrees = table.shape[1]
    parts = mixer.shape[0] // vectors
    return pl.pallas_call(
        functools.partial(finish_kernel, float(coefficients)),
        out_shape=(
            jax.ShapeDtypeStruct((vectors, orders, parts, degrees), BF16),
            jax.ShapeDtypeStruct((total, total), F32),
        ),
        in_specs=[pl.BlockSpec(memory_space=VMEM)] * 4,
        out_specs=(pl.BlockSpec(memory_space=pl.ANY), pl.BlockSpec(memory_space=VMEM)),
        scratch_shapes=[
            VMEM((total, 2 * total), F32),
            VMEM((orders, vectors, parts, degrees), BF16),
            DMA((orders,)),
        ],
        compiler_params=pltpu.CompilerParams(vmem_limit_bytes=32 * 1024 * 1024),
        name="finish",
    )(rows, ab, mixer, table)


def shards(trial_block, legendre, order_slot, cycle_start, cycle_count, cycle_weight):
    n_ma = lax.axis_size("ma")
    n_vert = lax.axis_size("vert")
    vectors, orders, parts, degrees = trial_block.shape
    trial = trial_block.reshape(vectors, orders, parts, degrees // LANES, LANES)
    trial = trial.transpose(0, 1, 3, 2, 4).reshape(vectors, orders, parts * degrees // LANES, LANES)
    terms = step_terms(
        trial, legendre, order_slot, cycle_start, cycle_count, cycle_weight, n_ma, n_vert
    )
    coefficients = order_slot.shape[0] * parts * degrees
    return finish(*terms, vectors, orders, coefficients)


def solution(mesh):
    in_specs = (P("vert", "ma", None, None), P("ma", None, None, None), P(), P(), P(), P())
    out_specs = (P("vert", "ma", None, None), P())
    return jax.shard_map(shards, mesh=mesh, in_specs=in_specs, out_specs=out_specs, check_vma=False)
```

profile of v0, /device:TPU:0, one launch (start us, length us, event | category | flops | bytes accessed | tf_op | source)
XLA Modules:
  0.0 60.9 jit_solution(4478235444500547366)
XLA Ops:
  0.6 49.6 %step_terms.1 = (f32[4,32,256]{2,1,0:T(8,128)}, f32[32,128]{1,0:T(8,128)}, bf16[128,256]{1,0:T(8,128)(2,1)}, bf16[128,1024]{1,0:T(8,128)(2,1)}) custom-call(bf16[32,8,32,128]{3,2,1,0:T(8,128)(2,1)} %bitcast.5, bf16[8,2,32,1024]{3,2,1,0:T(8,128)(2,1)} %legendre_ref.1, s32[64]{0:T(128)} %order_ref.1, s32[32]{0:T(128)} %start_ref.1, s32[32]{0:T(128)} %count_ref.1, ...), custom_call_target="tpu_custom_call" | custom-call | tf_op jit(solution)/shard_map/step_terms/pallas_call | solution.py:552
  50.3 0.0 copy-start
  50.3 0.9 %copy-done = bf16[128,1024]{1,0:T(8,128)(2,1)S(1)} copy-done((bf16[128,1024]{1,0:T(8,128)(2,1)S(1)}, bf16[128,1024]{1,0:T(8,128)(2,1)}, u32[]{:S(2)}) %copy-start) | copy-done | bytes 262168
  51.2 0.0 copy-start.1
  51.2 0.9 %copy-done.1 = f32[4,32,256]{2,1,0:T(8,128)S(1)} copy-done((f32[4,32,256]{2,1,0:T(8,128)S(1)}, f32[4,32,256]{2,1,0:T(8,128)}, u32[]{:S(2)}) %copy-start.1) | copy-done | bytes 131096
  52.1 0.0 copy-start.2
  52.1 0.8 %copy-done.2 = bf16[128,256]{1,0:T(8,128)(2,1)S(1)} copy-done((bf16[128,256]{1,0:T(8,128)(2,1)S(1)}, bf16[128,256]{1,0:T(8,128)(2,1)}, u32[]{:S(2)}) %copy-start.2) | copy-done | bytes 65560
  53.0 0.0 copy-start.3
  53.0 0.7 %copy-done.3 = f32[32,128]{1,0:T(8,128)S(1)} copy-done((f32[32,128]{1,0:T(8,128)S(1)}, f32[32,128]{1,0:T(8,128)}, u32[]{:S(2)}) %copy-start.3) | copy-done | bytes 16408
  53.7 7.2 %finish.1 = (bf16[32,8,4,1024]{3,2,1,0:T(4,128)(2,1)}, f32[128,128]{1,0:T(8,128)}) custom-call(f32[4,32,256]{2,1,0:T(8,128)S(1)} %copy-done.1, f32[32,128]{1,0:T(8,128)S(1)} %copy-done.3, bf16[128,256]{1,0:T(8,128)(2,1)S(1)} %copy-done.2, bf16[128,1024]{1,0:T(8,128)(2,1)S(1)} %copy-done), custom_call_target="tpu_custom_call" | custom-call | tf_op jit(solution)/shard_map/finish/pallas_call | solution.py:657
Async XLA Ops:
  50.3 1.0 %copy-start = (bf16[128,1024]{1,0:T(8,128)(2,1)S(1)}, bf16[128,1024]{1,0:T(8,128)(2,1)}, u32[]{:S(2)}) copy-start(bf16[128,1024]{1,0:T(8,128)(2,1)} %get-tuple-element.9.leg_ref) | copy-start | bytes 786436
  51.2 0.9 %copy-start.1 = (f32[4,32,256]{2,1,0:T(8,128)S(1)}, f32[4,32,256]{2,1,0:T(8,128)}, u32[]{:S(2)}) copy-start(f32[4,32,256]{2,1,0:T(8,128)} %get-tuple-element.6.rows_ref) | copy-start | bytes 393220
  52.1 0.8 %copy-start.2 = (bf16[128,256]{1,0:T(8,128)(2,1)S(1)}, bf16[128,256]{1,0:T(8,128)(2,1)}, u32[]{:S(2)}) copy-start(bf16[128,256]{1,0:T(8,128)(2,1)} %get-tuple-element.8.mixer_ref) | copy-start | bytes 196612
  53.0 0.7 %copy-start.3 = (f32[32,128]{1,0:T(8,128)S(1)}, f32[32,128]{1,0:T(8,128)}, u32[]{:S(2)}) copy-start(f32[32,128]{1,0:T(8,128)} %get-tuple-element.7.ab_ref) | copy-start | bytes 49156
where the time goes:
time: 61.2 us; the launch traced here: 60.9 us
  Pallas kernels  56.8 us (93%)
  local copies, waits for them, and re-layouts  3.4 us (6%)
  between operations  0.65 us (1%)
    pallas_call x1, Pallas kernels, step_terms(): pl.pallas_call(functools.partial(step_kernel, n_ma, n_vert, live), out_sh...  49.6 us
    pallas_call x1, Pallas kernels, finish(): pl.pallas_call(functools.partial(finish_kernel, float(coefficients)), out...  7.18 us
    unnamed x8, local copies, waits for them, and re-layouts  3.4 us

commit v1 on v0

--- a/solution.py
+++ b/solution.py
@@ -16,11 +16,11 @@
 BF16 = jnp.bfloat16
 I32 = jnp.int32
 HIGHEST = lax.Precision.HIGHEST
-GRANT = 60 * 1024 * 1024
+MIB = 1024 * 1024
 LANES = 128
 PANEL = 16
 NT = (((1,), (1,)), ((), ()))
-STAGES = (7, 12)
+STAGES = (7, 13)
 
 
 def iota(shape, axis):
@@ -100,25 +100,26 @@
 
 def step_kernel(
     n_ma, n_vert, live,
-    trial_ref, legendre_ref, order_ref, start_ref, count_ref, weight_ref,
+    trial_ref, legendre_ref, order_in, start_in, count_in, weight_in,
     rows_ref, ab_ref, mixer_ref, leg_ref,
-    native, leg_in, near, far, message, gathered, spectra, returned, packed,
+    native, leg_in, mine, theirs, far, message, gathered, spectra, returned, packed,
     row_a, land_a, sum_a, row_b, land_b, ab_own, land_c, ab_mid, land_d,
     work, lhs, llm, tables, back_table,
-    load_sem, leg_sem, near_send, near_recv, far_send, far_recv,
+    order_ref, start_ref, count_ref, weight_ref,
+    load_sem, leg_sem, small_sem, near_send, near_recv, far_send, far_recv,
     ma_send, ma_recv, vert_send, vert_recv,
 ):
     ma = lax.axis_index("ma")
     vert = lax.axis_index("vert")
-    pairs, vectors, _, per, _ = native.shape
-    orders = 2 * pairs
-    parts, degrees = near.shape[2], near.shape[4]
+    _, vectors, share, per, _ = native.shape
+    orders = n_vert * share
+    parts, degrees = mine.shape[2], mine.shape[4]
     tiles = degrees // LANES
     cycles = leg_in.shape[2]
     half = n_vert // 2
-    share = orders // n_vert
     place = lax.rem(vert, half)
     side = vert // half
+    assert half == 2
     total = n_vert * vectors
     terms = live * orders
     longitudes = 2 * n_ma * orders
@@ -142,91 +143,70 @@
     lax.fori_loop(1, n_ma, greet_ma, 0)
     lax.fori_loop(1, n_vert, greet_vert, 0)
 
-    def load(pair):
-        at = pl.ds(2 * pair, 2)
-        return pltpu.make_async_copy(trial_ref.at[:, at], native.at[pair], load_sem.at[pair])
-
-    def pair_at(i):
-        return lax.rem((1 - side) * (orders // 4) + i, orders // 2)
-
-    for i in range(orders // 2):
-        load(pair_at(i)).start()
+    def pair_at(i, place=place):
+        group = 1 - side if i < half else side
+        return group * half + lax.rem(place + i, half)
+
+    def load(i):
+        at = pl.ds(pair_at(i) * share, share)
+        return pltpu.make_async_copy(trial_ref.at[:, at], native.at[i], load_sem.at[i])
+
     leg_copy = pltpu.make_async_copy(legendre_ref, leg_in, leg_sem)
-    leg_copy.start()
+    small = [(order_in, order_ref), (start_in, start_ref), (count_in, count_ref), (weight_in, weight_ref)]
+    small = [pltpu.make_async_copy(*pair, small_sem.at[n]) for n, pair in enumerate(small)]
+    for copy in small:
+        copy.start()
+    for i in range(n_vert):
+        load(i).start()
+        if i == half - 1:
+            leg_copy.start()
 
     rows = 8 * per
     row = iota((rows, rows), 0)
     column = iota((rows, rows), 1)
-    wanted = lax.rem(row, 8) * per + lax.rem(row // 8, tiles) * parts + row // (8 * tiles)
+    wanted = modulo(row, 8) * per + modulo(row // 8, tiles) * parts + row // (8 * tiles)
     reorder = (column == wanted).astype(BF16)
 
-    for i in range(orders // 2):
-        load(pair_at(i)).wait()
-    leg_copy.wait()
-
-    def arrange(i, carry):
-        pair = pair_at(i)
+    def arrange(i):
+        load(i).wait()
         for g in range(vectors // 16):
-            blocks = []
-            for h in range(2):
-                at = pl.ds(16 * g + 8 * h, 8)
-                both = [native[pair, at, e].reshape(rows, LANES) for e in range(2)]
-                blocks.append(mm(reorder, jnp.concatenate(both, axis=1)))
-            for e in range(2):
-                for c in range(parts):
-                    for t in range(tiles):
-                        lo = (c * tiles + t) * 8
-                        at = (slice(lo, lo + 8), slice(e * LANES, (e + 1) * LANES))
-                        tile = jnp.concatenate([blocks[0][at], blocks[1][at]], axis=0)
-                        at = (slice(16 * g, 16 * g + 16), slice(t * LANES, (t + 1) * LANES))
-                        near[(place, 2 * pair + e, c) + at] = tile.astype(BF16)
-        return carry
-
-    lax.fori_loop(0, orders // 2, arrange, 0)
-
-    def search(i, found):
-        j = cycles - 1 - i
-        return jnp.where(count_ref[j] > 0, j, found)
-
-    first = jnp.minimum(lax.fori_loop(0, cycles, search, 0), cycles - live)
-
-    block = min(terms, 64)
-    for kind in range(2):
-        source = leg_in[:, kind].reshape(orders * cycles, degrees)
-
-        def pick(i, carry):
-            row = iota((block, orders * cycles), 0) + i * block
-            column = iota((block, orders * cycles), 1)
-            wanted = lax.rem(row, orders) * cycles + row // orders + first
-            at = rows_at(kind * (terms // block) + i, block)
-            leg_ref[at, :] = mm((column == wanted).astype(BF16), source).astype(BF16)
-            return carry
-
-        lax.fori_loop(0, terms // block, pick, 0)
-
-    pl.semaphore_wait(barrier, n_ma + n_vert - 2)
-
-    def near_copy(peer, slot, source):
+            for e in range(0, share, 2):
+                blocks = []
+                for h in range(2):
+                    at = pl.ds(16 * g + 8 * h, 8)
+                    both = [native[i, at, e + n].reshape(rows, LANES) for n in range(2)]
+                    blocks.append(mm(reorder, jnp.concatenate(both, axis=1)))
+                for n in range(2):
+                    for c in range(parts):
+                        for t in range(tiles):
+                            lo = (c * tiles + t) * 8
+                            at = (slice(lo, lo + 8), slice(n * LANES, (n + 1) * LANES))
+                            tile = jnp.concatenate([blocks[0][at], blocks[1][at]], axis=0)
+                            at = (slice(16 * g, 16 * g + 16), slice(t * LANES, (t + 1) * LANES))
+                            mine[(i, e + n, c) + at] = tile.astype(BF16)
+
+    def near_copy(i, source):
         return pltpu.make_async_remote_copy(
-            src_ref=near.at[source],
-            dst_ref=near.at[source],
-            send_sem=near_send.at[slot],
-            recv_sem=near_recv.at[slot],
-            device_id=(ma, peer),
+            src_ref=mine.at[i],
+            dst_ref=theirs.at[pair_at(i, source)],
+            send_sem=near_send.at[i],
+            recv_sem=near_recv.at[i],
+            device_id=(ma, side * half + 1 - place),
             device_id_type=MESH,
         )
 
-    pieces = half * share * parts
+    each = share * parts
+    pieces = half * each
 
     def far_copy(piece, arriving=False):
-        offset = lax.rem(piece, half)
-        inner = piece // half
+        offset = piece // each
+        inner = lax.rem(piece, each)
         peer = (1 - side) * half + lax.rem(place + offset, half)
         slot = lax.rem(place + half - offset, half) if arriving else place
         s = inner // parts
         c = lax.rem(inner, parts)
         return pltpu.make_async_remote_copy(
-            src_ref=near.at[slot, peer * share + s, c],
+            src_ref=mine.at[offset, s, c],
             dst_ref=far.at[slot, s, c],
             send_sem=far_send.at[piece],
             recv_sem=far_recv.at[piece],
@@ -242,19 +222,50 @@
         lax.fori_loop(begin, end, body, 0)
 
     cuts = [min(pieces, cut) for cut in STAGES]
-    send_far(0, cuts[0])
-    for step in range(1, half):
-        near_copy(side * half + lax.rem(place + step, half), step, place).start()
+    arrange(0)
+    pl.semaphore_wait(barrier, n_ma + n_vert - 2)
+    send_far(0, min(each, cuts[0]))
+    for i in range(1, half):
+        arrange(i)
+    if cuts[0] > each:
+        send_far(each, cuts[0])
+
+    for copy in small:
+        copy.wait()
+
+    def search(i, found):
+        j = cycles - 1 - i
+        return jnp.where(count_ref[j] > 0, j, found)
+
+    first = jnp.minimum(lax.fori_loop(0, cycles, search, 0), cycles - live)
+
+    leg_copy.wait()
+    block = min(terms, 64)
+    for kind in range(2):
+        source = leg_in[:, kind].reshape(orders * cycles, degrees)
+
+        def pick(i, carry):
+            row = iota((block, orders * cycles), 0) + i * block
+            column = iota((block, orders * cycles), 1)
+            wanted = modulo(row, orders) * cycles + row // orders + first
+            at = rows_at(kind * (terms // block) + i, block)
+            leg_ref[at, :] = mm((column == wanted).astype(BF16), source).astype(BF16)
+            return carry
+
+        lax.fori_loop(0, terms // block, pick, 0)
+
+    for i in range(half, n_vert):
+        arrange(i)
+    for i in range(n_vert):
+        near_copy(i, place).start()
 
     keep = lax.rem(iota((2 * terms, LANES), 0), orders)
 
-    def product(s, carry):
-        vectors_here = near[place, s].reshape(parts * vectors, degrees)
-        found = mm_nt(leg_ref[...], vectors_here)
-        spectra[...] = jnp.where(keep == s, found, spectra[...])
-        return carry
-
-    lax.fori_loop(0, orders, product, 0)
+    for i in range(n_vert):
+        for e in range(share):
+            found = mm_nt(leg_ref[...], mine[i, e].reshape(parts * vectors, degrees))
+            here = keep == pair_at(i) * share + e
+            spectra[...] = jnp.where(here, found, spectra[...]) if i + e else found
     w = spectra[:terms, :]
     x = spectra[terms:, :]
     quarter = iota((terms, LANES), 1) // vectors
@@ -375,16 +386,18 @@
     phase = phase + jnp.where(row >= orders, longitudes - longitudes // 4, 0)
     back_table[...] = (cosines(modulo(phase, longitudes), longitudes) * scale).astype(BF16)
 
-    for step in range(1, half):
-        peer = side * half + lax.rem(place + step, half)
-        near_copy(peer, half - step, lax.rem(place + step, half)).wait_recv()
-
-    def near_gram(s, sums):
-        for c in range(parts):
-            sums = sums + mm_nt(near[place, s, c], near[:, s, c].reshape(half * vectors, degrees))
-        return sums
-
-    near_sums = lax.fori_loop(0, orders, near_gram, jnp.zeros((vectors, half * vectors), F32))
+    for i in range(n_vert):
+        near_copy(i, 1 - place).wait_recv()
+    near_sums = jnp.zeros((vectors, half * vectors), F32)
+    for i in range(n_vert):
+        for e in range(share):
+            for c in range(parts):
+                here = mine[i, e, c]
+                both = jnp.concatenate([here, theirs[pair_at(i), e, c]], axis=0)
+                near_sums = near_sums + mm_nt(here, both)
+    first_half, second_half = near_sums[:, :vectors], near_sums[:, vectors:]
+    swapped = jnp.concatenate([second_half, first_half], axis=1)
+    near_sums = jnp.where(place == 0, near_sums, swapped)
     row_b[:, total:] = jnp.concatenate([near_sums, jnp.zeros_like(near_sums)], axis=1)
 
     ma_wait(0, message, gathered)
@@ -451,16 +464,12 @@
     ma_start(1, row_a, land_a)
     land_a[ma] = row_a[...]
     row_b[:, :total] = found[3] + found[4] + found[5]
-    ma_start(2, row_b, land_b)
     land_b[ma] = row_b[...]
     ma_wait(1, row_a, land_a)
     sum_a[vert] = jnp.sum(land_a[...], axis=0)
     vert_start(1, sum_a.at[vert], sum_a)
-    ma_wait(2, row_b, land_b)
-    rows_ref[vert] = jnp.sum(land_b[...], axis=0)
-    vert_start(2, rows_ref.at[vert], rows_ref)
     send_far(cuts[1], pieces)
-
+    ma_start(2, row_b, land_b)
     vert_wait(1, sum_a.at[vert], sum_a)
     inverse_count = 1.0 / (n_ma * orders * parts * degrees)
     work[:, :total] = sum_a[...].reshape(total, total) * inverse_count
@@ -472,6 +481,9 @@
 
     panels = total // PANEL
     lax.fori_loop(0, panels // 2, panel_step, 0)
+    ma_wait(2, row_b, land_b)
+    rows_ref[vert] = jnp.sum(land_b[...], axis=0)
+    vert_start(2, rows_ref.at[vert], rows_ref)
 
     def far_wait(piece, carry):
         far_copy(piece, True).wait_recv()
@@ -479,15 +491,14 @@
 
     lax.fori_loop(0, pieces, far_wait, 0)
 
-    def far_gram(s, sums):
+    cross_sums = jnp.zeros((half * vectors, half * vectors), F32)
+    for e in range(share):
         for c in range(parts):
-            here = near[:, vert * share + s, c].reshape(half * vectors, degrees)
-            sums = sums + mm_nt(here, far[:, s, c].reshape(half * vectors, degrees))
-        return sums
-
-    cross_sums = lax.fori_loop(
-        0, share, far_gram, jnp.zeros((half * vectors, half * vectors), F32)
-    )
+            here = jnp.concatenate([mine[half, e, c], theirs[vert, e, c]], axis=0)
+            there = far[:, e, c].reshape(half * vectors, degrees)
+            cross_sums = cross_sums + mm_nt(here, there)
+    swapped = jnp.concatenate([cross_sums[vectors:], cross_sums[:vectors]], axis=0)
+    cross_sums = jnp.where(place == 0, cross_sums, swapped)
     cross_sums = jnp.where(side == 0, cross_sums, cross_sums.T)
     size = half * vectors
     ab_own[...] = jnp.concatenate([cross_sums[: size // 2], cross_sums[size // 2 :]], axis=1)
@@ -518,8 +529,8 @@
     ma_wait(3, ab_mid, land_d)
     ab_ref[...] = jnp.sum(land_d[...], axis=0)
 
-    for step in range(1, half):
-        near_copy(side * half + lax.rem(place + step, half), step, place).wait_send()
+    for i in range(n_vert):
+        near_copy(i, place).wait_send()
 
     def far_done(piece, carry):
         far_copy(piece).wait_send()
@@ -548,7 +559,8 @@
     longitudes = 2 * n_ma * orders
     pieces = half * share * parts
     columns = live * 2 * vectors
-    anywhere = pl.BlockSpec(memory_space=pl.ANY)
+    grant = min(60, 16 + terms // 16) * MIB
+    anywhere = pl.BlockSpec(memory_space=pltpu.HBM)
     return pl.pallas_call(
         functools.partial(step_kernel, n_ma, n_vert, live),
         out_shape=(
@@ -557,12 +569,13 @@
             jax.ShapeDtypeStruct((parts * vectors, 4 * terms), BF16),
             jax.ShapeDtypeStruct((2 * terms, degrees), BF16),
         ),
-        in_specs=[anywhere, anywhere] + [pl.BlockSpec(memory_space=SMEM)] * 4,
+        in_specs=[anywhere] * 6,
         out_specs=[pl.BlockSpec(memory_space=VMEM)] * 4,
         scratch_shapes=[
-            VMEM((orders // 2, vectors, 2, per, LANES), BF16),
+            VMEM((n_vert, vectors, share, per, LANES), BF16),
             VMEM(legendre.shape, BF16),
-            VMEM((half, orders, parts, vectors, degrees), BF16),
+            VMEM((n_vert, share, parts, vectors, degrees), BF16),
+            VMEM((n_vert, share, parts, vectors, degrees), BF16),
             VMEM((half, share, parts, vectors, degrees), BF16),
             VMEM((2 * orders, columns), BF16),
             VMEM((n_ma, 2 * orders, columns), BF16),
@@ -583,10 +596,15 @@
             VMEM((3, 2 * terms, 2 * terms), BF16),
             VMEM((longitudes, n_ma * 2 * orders), BF16),
             VMEM((2 * orders, longitudes), BF16),
-            DMA((orders // 2,)),
+            SMEM(order_slot.shape, I32),
+            SMEM(cycle_start.shape, I32),
+            SMEM(cycle_count.shape, I32),
+            SMEM(cycle_weight.shape, F32),
+            DMA((n_vert,)),
             DMA,
-            DMA((half,)),
-            DMA((half,)),
+            DMA((4,)),
+            DMA((n_vert,)),
+            DMA((n_vert,)),
             DMA((pieces,)),
             DMA((pieces,)),
             DMA((4, n_ma)),
@@ -595,7 +613,7 @@
             DMA((4, n_vert)),
         ],
         compiler_params=pltpu.CompilerParams(
-            collective_id=0, has_side_effects=True, vmem_limit_bytes=GRANT
+            collective_id=0, has_side_effects=True, vmem_limit_bytes=grant
         ),
         name="step_terms",
     )(trial, legendre, order_slot, cycle_start, cycle_count, cycle_weight)
@@ -678,9 +696,9 @@
     vectors, orders, parts, degrees = trial_block.shape
     trial = trial_block.reshape(vectors, orders, parts, degrees // LANES, LANES)
     trial = trial.transpose(0, 1, 3, 2, 4).reshape(vectors, orders, parts * degrees // LANES, LANES)
-    terms = step_terms(
-        trial, legendre, order_slot, cycle_start, cycle_count, cycle_weight, n_ma, n_vert
-    )
+    inputs = (trial, legendre, order_slot, cycle_start, cycle_count, cycle_weight)
+    inputs = [pltpu.with_memory_space_constraint(x, pltpu.HBM) for x in inputs]
+    terms = step_terms(*inputs, n_ma, n_vert)
     coefficients = order_slot.shape[0] * parts * degrees
     return finish(*terms, vectors, orders, coefficients)
 

time: 61.2 us -> 48.2 us (0.79)
  Pallas kernels: 56.8 us -> 47.4 us
  local copies, waits for them, and re-layouts: 3.4 us -> 0 us
    pallas_call x1, Pallas kernels: 49.6 us -> 40.2 us  [step_terms(): pl.pallas_call(functools.partial(step_kernel, n_ma, n_vert, live), out_sh...]
    unnamed x8 -> x0, local copies, waits for them, and re-layouts: 3.4 us -> none
where the time goes in v1:
time: 48.2 us; the launch traced here: 48 us
  Pallas kernels  47.4 us (98%)
  between operations  0.64 us (1%)
    pallas_call x1, Pallas kernels, step_terms(): pl.pallas_call(functools.partial(step_kernel, n_ma, n_vert, live), out_sh...  40.2 us
    pallas_call x1, Pallas kernels, finish(): pl.pallas_call(functools.partial(finish_kernel, float(coefficients)), out...  7.18 us

profile of v1, /device:TPU:0, one launch (start us, length us, event | category | flops | bytes accessed | tf_op | source)
XLA Modules:
  0.0 48.0 jit_solution(13004947299783746366)
XLA Ops:
  0.6 40.2 %step_terms.1 = (f32[4,32,256]{2,1,0:T(8,128)S(1)}, f32[32,128]{1,0:T(8,128)S(1)}, bf16[128,256]{1,0:T(8,128)(2,1)S(1)}, bf16[128,1024]{1,0:T(8,128)(2,1)S(1)}) custom-call(bf16[32,8,32,128]{3,2,1,0:T(8,128)(2,1)} %bitcast.5, bf16[8,2,32,1024]{3,2,1,0:T(8,128)(2,1)} %legendre_ref.1, s32[64]{0:T(128)} %order_in.1, s32[32]{0:T(128)} %start_in.1, s32[32]{0:T(128)} %count_in.1, ...), custom_call_target="tpu_custom_call" | custom-call | tf_op jit(solution)/shard_map/step_terms/pallas_call | solution.py:564
  40.8 7.2 %finish.1 = (bf16[32,8,4,1024]{3,2,1,0:T(4,128)(2,1)}, f32[128,128]{1,0:T(8,128)}) custom-call(f32[4,32,256]{2,1,0:T(8,128)S(1)} %get-tuple-element.6.rows_ref, f32[32,128]{1,0:T(8,128)S(1)} %get-tuple-element.7.ab_ref, bf16[128,256]{1,0:T(8,128)(2,1)S(1)} %get-tuple-element.8.mixer_ref, bf16[128,1024]{1,0:T(8,128)(2,1)S(1)} %get-tuple-element.9.leg_ref), custom_call_target="tpu_custom_call" | custom-call | tf_op jit(solution)/shard_map/finish/pallas_call | solution.py:675

commit v2 on v1

--- a/solution.py
+++ b/solution.py
@@ -20,7 +20,7 @@
 LANES = 128
 PANEL = 16
 NT = (((1,), (1,)), ((), ()))
-STAGES = (7, 13)
+STAGES = (6, 12, 16)
 
 
 def iota(shape, axis):
@@ -57,11 +57,11 @@
 
 
 def factor_panel(work, p):
-    size = work.shape[0]
+    size, width = work.shape
     first = pl.multiple_of(p * PANEL, PANEL)
     at = pl.ds(first, PANEL)
     lane = iota((PANEL, size), 1)
-    sub = iota((PANEL, 2 * size), 0)
+    sub = iota((PANEL, width), 0)
     x = work[at, :]
     column = [
         jnp.sum(jnp.where(lane == first + i, x[:, :size], 0.0), axis=1, keepdims=True)
@@ -78,7 +78,7 @@
         x[:, :size], x, (((0,), (0,)), ((), ())),
         precision=HIGHEST, preferred_element_type=F32,
     )
-    below = iota((size, 2 * size), 0) >= first + PANEL
+    below = iota((size, width), 0) >= first + PANEL
     work[...] = jnp.where(below, work[...] - update, work[...])
     work[at, :] = x
 
@@ -101,10 +101,10 @@
 def step_kernel(
     n_ma, n_vert, live,
     trial_ref, legendre_ref, order_in, start_in, count_in, weight_in,
-    rows_ref, ab_ref, mixer_ref, leg_ref,
-    native, leg_in, mine, theirs, far, message, gathered, spectra, returned, packed,
-    row_a, land_a, sum_a, row_b, land_b, ab_own, land_c, ab_mid, land_d,
-    work, lhs, llm, tables, back_table,
+    cross_ref, corner_ref, ab_ref, basis_ref,
+    leg_ref, native, leg_in, mine, theirs, far, message, gathered, spectra, returned, packed,
+    row_a, land_a, sum_a, row_b, land_b, sum_b, row_e, land_e, sum_e, ab_own, land_c, ab_mid, land_d,
+    work, corner, lhs, llm, tables, back_table,
     order_ref, start_ref, count_ref, weight_ref,
     load_sem, leg_sem, small_sem, near_send, near_recv, far_send, far_recv,
     ma_send, ma_recv, vert_send, vert_recv,
@@ -262,8 +262,9 @@
     keep = lax.rem(iota((2 * terms, LANES), 0), orders)
 
     for i in range(n_vert):
+        both = mm_nt(leg_ref[...], mine[i].reshape(share * parts * vectors, degrees))
         for e in range(share):
-            found = mm_nt(leg_ref[...], mine[i, e].reshape(parts * vectors, degrees))
+            found = both[:, e * LANES : (e + 1) * LANES]
             here = keep == pair_at(i) * share + e
             spectra[...] = jnp.where(here, found, spectra[...]) if i + e else found
     w = spectra[:terms, :]
@@ -385,20 +386,6 @@
     phase = iota((2 * orders, longitudes), 1) * own_order
     phase = phase + jnp.where(row >= orders, longitudes - longitudes // 4, 0)
     back_table[...] = (cosines(modulo(phase, longitudes), longitudes) * scale).astype(BF16)
-
-    for i in range(n_vert):
-        near_copy(i, 1 - place).wait_recv()
-    near_sums = jnp.zeros((vectors, half * vectors), F32)
-    for i in range(n_vert):
-        for e in range(share):
-            for c in range(parts):
-                here = mine[i, e, c]
-                both = jnp.concatenate([here, theirs[pair_at(i), e, c]], axis=0)
-                near_sums = near_sums + mm_nt(here, both)
-    first_half, second_half = near_sums[:, :vectors], near_sums[:, vectors:]
-    swapped = jnp.concatenate([second_half, first_half], axis=1)
-    near_sums = jnp.where(place == 0, near_sums, swapped)
-    row_b[:, total:] = jnp.concatenate([near_sums, jnp.zeros_like(near_sums)], axis=1)
 
     ma_wait(0, message, gathered)
     columns = message.shape[1]
@@ -463,13 +450,42 @@
     row_a[...] = found[0] + found[1] + found[2]
     ma_start(1, row_a, land_a)
     land_a[ma] = row_a[...]
-    row_b[:, :total] = found[3] + found[4] + found[5]
+    row_b[...] = found[3] + found[4] + found[5]
     land_b[ma] = row_b[...]
+
+    for i in range(n_vert):
+        near_copy(i, 1 - place).wait_recv()
+    wide = parts * vectors
+    near_sums = jnp.zeros((wide, 2 * wide), F32)
+    for i in range(n_vert):
+        for e in range(share):
+            here = mine[i, e].reshape(wide, degrees)
+            both = jnp.concatenate([here, theirs[pair_at(i), e].reshape(wide, degrees)], axis=0)
+            near_sums = near_sums + mm_nt(here, both)
+    first_half, second_half = [
+        sum(
+            near_sums[c * vectors : (c + 1) * vectors, n * wide + c * vectors : n * wide + (c + 1) * vectors]
+            for c in range(parts)
+        )
+        for n in range(2)
+    ]
+    near_sums = jnp.concatenate([first_half, second_half], axis=1)
+    swapped = jnp.concatenate([second_half, first_half], axis=1)
+    near_sums = jnp.where(place == 0, near_sums, swapped)
+    row_e[...] = jnp.concatenate([near_sums[: vectors // 2], near_sums[vectors // 2 :]], axis=1)
+    ma_start(4, row_e, land_e)
+    land_e[ma] = row_e[...]
+
     ma_wait(1, row_a, land_a)
     sum_a[vert] = jnp.sum(land_a[...], axis=0)
     vert_start(1, sum_a.at[vert], sum_a)
-    send_far(cuts[1], pieces)
+    send_far(cuts[1], cuts[2])
     ma_start(2, row_b, land_b)
+    ma_wait(4, row_e, land_e)
+    sum_e[vert] = jnp.sum(land_e[...], axis=0)
+    vert_start(4, sum_e.at[vert], sum_e)
+    send_far(cuts[2], pieces)
+
     vert_wait(1, sum_a.at[vert], sum_a)
     inverse_count = 1.0 / (n_ma * orders * parts * degrees)
     work[:, :total] = sum_a[...].reshape(total, total) * inverse_count
@@ -480,10 +496,10 @@
         return carry
 
     panels = total // PANEL
-    lax.fori_loop(0, panels // 2, panel_step, 0)
+    lax.fori_loop(0, panels, panel_step, 0)
+
     ma_wait(2, row_b, land_b)
-    rows_ref[vert] = jnp.sum(land_b[...], axis=0)
-    vert_start(2, rows_ref.at[vert], rows_ref)
+    sum_b[vert] = jnp.sum(land_b[...], axis=0)
 
     def far_wait(piece, carry):
         far_copy(piece, True).wait_recv()
@@ -491,12 +507,30 @@
 
     lax.fori_loop(0, pieces, far_wait, 0)
 
-    cross_sums = jnp.zeros((half * vectors, half * vectors), F32)
+    cross_sums = jnp.zeros((2 * wide, 2 * wide), F32)
     for e in range(share):
-        for c in range(parts):
-            here = jnp.concatenate([mine[half, e, c], theirs[vert, e, c]], axis=0)
-            there = far[:, e, c].reshape(half * vectors, degrees)
-            cross_sums = cross_sums + mm_nt(here, there)
+        here = [mine[half, e].reshape(wide, degrees), theirs[vert, e].reshape(wide, degrees)]
+        there = far[:, e].reshape(half * wide, degrees)
+        cross_sums = cross_sums + mm_nt(jnp.concatenate(here, axis=0), there)
+    cross_sums = jnp.concatenate(
+        [
+            jnp.concatenate(
+                [
+                    sum(
+                        cross_sums[
+                            m * wide + c * vectors : m * wide + (c + 1) * vectors,
+                            n * wide + c * vectors : n * wide + (c + 1) * vectors,
+                        ]
+                        for c in range(parts)
+                    )
+                    for n in range(2)
+                ],
+                axis=1,
+            )
+            for m in range(2)
+        ],
+        axis=0,
+    )
     swapped = jnp.concatenate([cross_sums[vectors:], cross_sums[:vectors]], axis=0)
     cross_sums = jnp.where(place == 0, cross_sums, swapped)
     cross_sums = jnp.where(side == 0, cross_sums, cross_sums.T)
@@ -504,11 +538,32 @@
     ab_own[...] = jnp.concatenate([cross_sums[: size // 2], cross_sums[size // 2 :]], axis=1)
     vert_start(3, ab_own, land_c)
     land_c[vert] = ab_own[...]
-    lax.fori_loop(panels // 2, panels, panel_step, 0)
+
+    vert_wait(4, sum_e.at[vert], sum_e)
+    blocks = sum_e[...]
+    size = half * vectors
+    near_blocks = [
+        jnp.concatenate([blocks[n][:, :size], blocks[n][:, size:]], axis=0) * inverse_count
+        for n in range(n_vert)
+    ]
+    diagonals = [jnp.concatenate(near_blocks[n * half : (n + 1) * half], axis=0) for n in range(2)]
+    unit = (iota((size, size), 0) == iota((size, size), 1)).astype(F32)
+    corner[...] = jnp.concatenate([diagonals[0], unit], axis=1)
+
+    def corner_step(p, carry):
+        factor_panel(corner, p)
+        return carry
+
+    lax.fori_loop(0, size // PANEL, corner_step, 0)
+    in_front = iota(corner.shape, 1) < size
+    inverse = jnp.where(in_front, swap(corner[...]), 0.0)
+    corner_ref[...] = jnp.concatenate([inverse[:, :size], diagonals[1]], axis=1)
+
     vert_wait(3, ab_own, land_c)
     ab_mid[...] = jnp.sum(land_c[...], axis=0)
     ma_start(3, ab_mid, land_d)
     land_d[ma] = ab_mid[...]
+    vert_start(2, sum_b.at[vert], sum_b)
 
     mixing = work[rows_at(vert, vectors), total:].astype(BF16)
     spread = (iota((parts * vectors, vectors), 0) // parts == iota((parts * vectors, vectors), 1))
@@ -521,13 +576,29 @@
         kind == 0, mixed_x * sign,
         jnp.where(kind == 1, mixed_y, jnp.where(kind == 2, -swap(mixed_y), -swap(mixed_x) * sign)),
     )
-    high, low = split(mixer, 2)
-    mixer_ref[:, : 2 * terms] = high
-    mixer_ref[:, 2 * terms :] = low
-
-    vert_wait(2, rows_ref.at[vert], rows_ref)
+    pieces_of = split(mixer, 2)
+    lane_order = modulo(iota(mixer.shape, 1), orders)
+
+    def mix(s, carry):
+        chosen = [jnp.where(lane_order == s, piece, jnp.zeros_like(piece)) for piece in pieces_of]
+        mixed = mm(chosen[0], leg_ref[...]) + mm(chosen[1], leg_ref[...])
+        basis_ref[:, s] = mixed.reshape(vectors, parts, degrees).astype(BF16)
+        return carry
+
+    lax.fori_loop(0, orders, mix, 0)
+
+    vert_wait(2, sum_b.at[vert], sum_b)
+    lower = (iota((size, total), 0) + size == iota((size, total), 1)).astype(F32)
+    outer = jnp.concatenate([inverse, lower], axis=0)
+    crossed = jnp.dot(
+        outer, sum_b[...].reshape(total, total) * inverse_count,
+        precision=HIGHEST, preferred_element_type=F32,
+    )
+    cross_ref[...] = lax.dot_general(
+        crossed, outer, NT, precision=HIGHEST, preferred_element_type=F32
+    )
     ma_wait(3, ab_mid, land_d)
-    ab_ref[...] = jnp.sum(land_d[...], axis=0)
+    ab_ref[...] = jnp.sum(land_d[...], axis=0) * inverse_count
 
     for i in range(n_vert):
         near_copy(i, place).wait_send()
@@ -542,7 +613,9 @@
     ma_done(1, row_a, land_a)
     ma_done(2, row_b, land_b)
     vert_done(1, sum_a.at[vert], sum_a)
-    vert_done(2, rows_ref.at[vert], rows_ref)
+    vert_done(2, sum_b.at[vert], sum_b)
+    ma_done(4, row_e, land_e)
+    vert_done(4, sum_e.at[vert], sum_e)
     vert_done(3, ab_own, land_c)
     ma_done(3, ab_mid, land_d)
 
@@ -564,14 +637,15 @@
     return pl.pallas_call(
         functools.partial(step_kernel, n_ma, n_vert, live),
         out_shape=(
-            jax.ShapeDtypeStruct((n_vert, vectors, total + 2 * half * vectors), F32),
+            jax.ShapeDtypeStruct((total, total), F32),
+            jax.ShapeDtypeStruct((half * vectors, 2 * half * vectors), F32),
             jax.ShapeDtypeStruct((half * vectors // 2, 2 * half * vectors), F32),
-            jax.ShapeDtypeStruct((parts * vectors, 4 * terms), BF16),
-            jax.ShapeDtypeStruct((2 * terms, degrees), BF16),
+            jax.ShapeDtypeStruct((vectors, orders, parts, degrees), BF16),
         ),
         in_specs=[anywhere] * 6,
         out_specs=[pl.BlockSpec(memory_space=VMEM)] * 4,
         scratch_shapes=[
+            VMEM((2 * terms, degrees), BF16),
             VMEM((n_vert, vectors, share, per, LANES), BF16),
             VMEM(legendre.shape, BF16),
             VMEM((n_vert, share, parts, vectors, degrees), BF16),
@@ -585,13 +659,18 @@
             VMEM((vectors, total), F32),
             VMEM((n_ma, vectors, total), F32),
             VMEM((n_vert, vectors, total), F32),
-            VMEM((vectors, total + 2 * half * vectors), F32),
-            VMEM((n_ma, vectors, total + 2 * half * vectors), F32),
+            VMEM((vectors, total), F32),
+            VMEM((n_ma, vectors, total), F32),
+            VMEM((n_vert, vectors, total), F32),
+            VMEM((vectors // 2, 2 * half * vectors), F32),
+            VMEM((n_ma, vectors // 2, 2 * half * vectors), F32),
+            VMEM((n_vert, vectors // 2, 2 * half * vectors), F32),
             VMEM((half * vectors // 2, 2 * half * vectors), F32),
             VMEM((n_vert, half * vectors // 2, 2 * half * vectors), F32),
             VMEM((half * vectors // 2, 2 * half * vectors), F32),
             VMEM((n_ma, half * vectors // 2, 2 * half * vectors), F32),
             VMEM((total, 2 * total), F32),
+            VMEM((half * vectors, 2 * half * vectors), F32),
             VMEM((6 * vectors, 4 * terms), BF16),
             VMEM((3, 2 * terms, 2 * terms), BF16),
             VMEM((longitudes, n_ma * 2 * orders), BF16),
@@ -607,10 +686,10 @@
             DMA((n_vert,)),
             DMA((pieces,)),
             DMA((pieces,)),
-            DMA((4, n_ma)),
-            DMA((4, n_ma)),
-            DMA((4, n_vert)),
-            DMA((4, n_vert)),
+            DMA((5, n_ma)),
+            DMA((5, n_ma)),
+            DMA((5, n_vert)),
+            DMA((5, n_vert)),
         ],
         compiler_params=pltpu.CompilerParams(
             collective_id=0, has_side_effects=True, vmem_limit_bytes=grant
@@ -619,75 +698,50 @@
     )(trial, legendre, order_slot, cycle_start, cycle_count, cycle_weight)
 
 
-def finish_kernel(
-    coefficients, rows_ref, ab_ref, mixer_ref, leg_ref, basis_ref, ritz_ref, work, staged, sems
-):
+def finish_kernel(cross_ref, corner_ref, ab_ref, staged_ref, basis_ref, ritz_ref, work, sem):
     total = ritz_ref.shape[0]
     size = total // 2
-    orders, vectors, parts, degrees = staged.shape
-    scale = 1.0 / coefficients
-    own = rows_ref[...].reshape(total, rows_ref.shape[2])
+    out = pltpu.make_async_copy(staged_ref, basis_ref, sem)
+    out.start()
     ab = ab_ref[...]
     ab = jnp.concatenate([ab[:, :size], ab[:, size:]], axis=0)
-    top = jnp.concatenate([own[:size, total : total + size], ab], axis=1)
-    bottom = jnp.concatenate([ab.T, own[size:, total : total + size]], axis=1)
-    work[:, :total] = jnp.concatenate([top, bottom], axis=0) * scale
-    work[:, total:] = (iota((total, total), 0) == iota((total, total), 1)).astype(F32)
-    mixer = mixer_ref[...]
-    lane_order = lax.rem(iota(mixer.shape, 1), orders)
-
-    def out_copy(s):
-        return pltpu.make_async_copy(staged.at[s], basis_ref.at[:, s], sems.at[s])
-
-    def mix(s):
-        picked = jnp.where(lane_order == s, mixer, jnp.zeros_like(mixer))
-        width = mixer.shape[1] // 2
-        mixed = mm(picked[:, :width], leg_ref[...]) + mm(picked[:, width:], leg_ref[...])
-        staged[s] = mixed.reshape(vectors, parts, degrees).astype(BF16)
-        out_copy(s).start()
-
-    panels = total // PANEL
-    assert panels == orders
+    inverse, diagonal = corner_ref[:, :size], corner_ref[:, size:]
+    beside = jnp.dot(inverse, ab, precision=HIGHEST, preferred_element_type=F32)
+    taken = lax.dot_general(
+        beside, beside, (((0,), (0,)), ((), ())), precision=HIGHEST, preferred_element_type=F32
+    )
+    unit = (iota((size, size), 0) == iota((size, size), 1)).astype(F32)
+    work[:, :total] = jnp.concatenate([diagonal - taken, jnp.zeros_like(unit)], axis=1)
+    work[:, total:] = jnp.concatenate([-beside.T, unit], axis=1)
 
     def step(p, carry):
         factor_panel(work, p)
-        mix(p)
-        return carry
-
-    lax.fori_loop(0, panels, step, 0)
-    inverse = work[:, total:]
-    half = jnp.dot(inverse, own[:, :total] * scale, precision=HIGHEST, preferred_element_type=F32)
+        return carry
+
+    lax.fori_loop(0, size // PANEL, step, 0)
+    upper = (iota((size, total), 0) == iota((size, total), 1)).astype(F32)
+    outer = jnp.concatenate([upper, work[:, total:]], axis=0)
+    crossed = jnp.dot(outer, cross_ref[...], precision=HIGHEST, preferred_element_type=F32)
     ritz_ref[...] = lax.dot_general(
-        half, inverse, NT, precision=HIGHEST, preferred_element_type=F32
+        crossed, outer, NT, precision=HIGHEST, preferred_element_type=F32
     )
-
-    def done(s, carry):
-        out_copy(s).wait()
-        return carry
-
-    lax.fori_loop(0, orders, done, 0)
-
-
-def finish(rows, ab, mixer, table, vectors, orders, coefficients):
-    total = rows.shape[0] * rows.shape[1]
-    degrees = table.shape[1]
-    parts = mixer.shape[0] // vectors
+    out.wait()
+
+
+def finish(cross, corner, ab, staged):
+    total = cross.shape[0]
     return pl.pallas_call(
-        functools.partial(finish_kernel, float(coefficients)),
+        finish_kernel,
         out_shape=(
-            jax.ShapeDtypeStruct((vectors, orders, parts, degrees), BF16),
+            jax.ShapeDtypeStruct(staged.shape, BF16),
             jax.ShapeDtypeStruct((total, total), F32),
         ),
         in_specs=[pl.BlockSpec(memory_space=VMEM)] * 4,
         out_specs=(pl.BlockSpec(memory_space=pl.ANY), pl.BlockSpec(memory_space=VMEM)),
-        scratch_shapes=[
-            VMEM((total, 2 * total), F32),
-            VMEM((orders, vectors, parts, degrees), BF16),
-            DMA((orders,)),
-        ],
-        compiler_params=pltpu.CompilerParams(vmem_limit_bytes=32 * 1024 * 1024),
+        scratch_shapes=[VMEM((total // 2, 2 * total), F32), DMA],
+        compiler_params=pltpu.CompilerParams(vmem_limit_bytes=8 * MIB),
         name="finish",
-    )(rows, ab, mixer, table)
+    )(cross, corner, ab, staged)
 
 
 def shards(trial_block, legendre, order_slot, cycle_start, cycle_count, cycle_weight):
@@ -698,9 +752,7 @@
     trial = trial.transpose(0, 1, 3, 2, 4).reshape(vectors, orders, parts * degrees // LANES, LANES)
     inputs = (trial, legendre, order_slot, cycle_start, cycle_count, cycle_weight)
     inputs = [pltpu.with_memory_space_constraint(x, pltpu.HBM) for x in inputs]
-    terms = step_terms(*inputs, n_ma, n_vert)
-    coefficients = order_slot.shape[0] * parts * degrees
-    return finish(*terms, vectors, orders, coefficients)
+    return finish(*step_terms(*inputs, n_ma, n_vert))
 
 
 def solution(mesh):

time: 48.2 us -> 46.1 us (0.956)
  Pallas kernels: 47.4 us -> 45.3 us
    pallas_call x1, Pallas kernels: 7.18 us -> 3.81 us  [finish(): pl.pallas_call(finish_kernel, out_shape=(jax.ShapeDtypeStruct(staged.shap...]
    pallas_call x1, Pallas kernels: 40.2 us -> 41.5 us  [step_terms(): pl.pallas_call(functools.partial(step_kernel, n_ma, n_vert, live), out_sh...]
where the time goes in v2:
time: 46.1 us; the launch traced here: 45.9 us
  Pallas kernels  45.3 us (98%)
  between operations  0.64 us (1%)
    pallas_call x1, Pallas kernels, step_terms(): pl.pallas_call(functools.partial(step_kernel, n_ma, n_vert, live), out_sh...  41.5 us
    pallas_call x1, Pallas kernels, finish(): pl.pallas_call(finish_kernel, out_shape=(jax.ShapeDtypeStruct(staged.shap...  3.81 us

profile of v2, /device:TPU:0, one launch (start us, length us, event | category | flops | bytes accessed | tf_op | source)
XLA Modules:
  0.0 45.9 jit_solution(6938719998084024086)
XLA Ops:
  0.6 41.5 %step_terms.1 = (f32[128,128]{1,0:T(8,128)S(1)}, f32[64,128]{1,0:T(8,128)S(1)}, f32[32,128]{1,0:T(8,128)S(1)}, bf16[32,8,4,1024]{3,2,1,0:T(4,128)(2,1)S(1)}) custom-call(bf16[32,8,32,128]{3,2,1,0:T(8,128)(2,1)} %bitcast.5, bf16[8,2,32,1024]{3,2,1,0:T(8,128)(2,1)} %legendre_ref.1, s32[64]{0:T(128)} %order_in.1, s32[32]{0:T(128)} %start_in.1, s32[32]{0:T(128)} %count_in.1, ...), custom_call_target="tpu_custom_call" | custom-call | tf_op jit(solution)/shard_map/step_terms/pallas_call | solution.py:637
  42.1 3.8 %finish.1 = (bf16[32,8,4,1024]{3,2,1,0:T(4,128)(2,1)}, f32[128,128]{1,0:T(8,128)}) custom-call(f32[128,128]{1,0:T(8,128)S(1)} %get-tuple-element.6.cross_ref, f32[64,128]{1,0:T(8,128)S(1)} %get-tuple-element.7.corner_ref, f32[32,128]{1,0:T(8,128)S(1)} %get-tuple-element.8.ab_ref, bf16[32,8,4,1024]{3,2,1,0:T(4,128)(2,1)S(1)} %get-tuple-element.9.staged_ref), custom_call_target="tpu_custom_call" | custom-call | tf_op jit(solution)/shard_map/finish/pallas_call | solution.py:733

commit v3 on v2

--- a/solution.py
+++ b/solution.py
@@ -20,7 +20,7 @@
 LANES = 128
 PANEL = 16
 NT = (((1,), (1,)), ((), ()))
-STAGES = (6, 12, 16)
+STAGES = (6, 13, 14)
 
 
 def iota(shape, axis):
@@ -74,9 +74,11 @@
             column[k] = column[k] - scaled * (column[k][i : i + 1, :] * inverse)
         line = x[i : i + 1, :] * inverse
         x = jnp.where(sub == i, line, jnp.where(sub > i, x - scaled * line, x))
+    high, middle, low = split(x, 3)
+    left = jnp.concatenate([high, high, high, middle, middle, low], axis=0)
+    right = jnp.concatenate([high, middle, low, high, middle, high], axis=0)
     update = lax.dot_general(
-        x[:, :size], x, (((0,), (0,)), ((), ())),
-        precision=HIGHEST, preferred_element_type=F32,
+        left[:, :size], right, (((0,), (0,)), ((), ())), preferred_element_type=F32
     )
     below = iota((size, width), 0) >= first + PANEL
     work[...] = jnp.where(below, work[...] - update, work[...])
@@ -496,7 +498,7 @@
         return carry
 
     panels = total // PANEL
-    lax.fori_loop(0, panels, panel_step, 0)
+    lax.fori_loop(0, panels // 2, panel_step, 0)
 
     ma_wait(2, row_b, land_b)
     sum_b[vert] = jnp.sum(land_b[...], axis=0)
@@ -550,11 +552,12 @@
     unit = (iota((size, size), 0) == iota((size, size), 1)).astype(F32)
     corner[...] = jnp.concatenate([diagonals[0], unit], axis=1)
 
-    def corner_step(p, carry):
+    def both_step(p, carry):
+        factor_panel(work, panels // 2 + p)
         factor_panel(corner, p)
         return carry
 
-    lax.fori_loop(0, size // PANEL, corner_step, 0)
+    lax.fori_loop(0, panels // 2, both_step, 0)
     in_front = iota(corner.shape, 1) < size
     inverse = jnp.where(in_front, swap(corner[...]), 0.0)
     corner_ref[...] = jnp.concatenate([inverse[:, :size], diagonals[1]], axis=1)

time: 46.1 us -> 45.1 us (0.978)
  Pallas kernels: 45.3 us -> 44.4 us
    pallas_call x1, Pallas kernels: 41.5 us -> 40.8 us  [step_terms(): pl.pallas_call(functools.partial(step_kernel, n_ma, n_vert, live), out_sh...]
where the time goes in v3:
time: 45.1 us; the launch traced here: 45 us
  Pallas kernels  44.4 us (98%)
  between operations  0.64 us (1%)
    pallas_call x1, Pallas kernels, step_terms(): pl.pallas_call(functools.partial(step_kernel, n_ma, n_vert, live), out_sh...  40.8 us
    pallas_call x1, Pallas kernels, finish(): pl.pallas_call(finish_kernel, out_shape=(jax.ShapeDtypeStruct(staged.shap...  3.53 us

profile of v3, /device:TPU:0, one launch (start us, length us, event | category | flops | bytes accessed | tf_op | source)
XLA Modules:
  0.0 45.0 jit_solution(11266872363097017447)
XLA Ops:
  0.6 40.8 %step_terms.1 = (f32[128,128]{1,0:T(8,128)S(1)}, f32[64,128]{1,0:T(8,128)S(1)}, f32[32,128]{1,0:T(8,128)S(1)}, bf16[32,8,4,1024]{3,2,1,0:T(4,128)(2,1)S(1)}) custom-call(bf16[32,8,32,128]{3,2,1,0:T(8,128)(2,1)} %bitcast.5, bf16[8,2,32,1024]{3,2,1,0:T(8,128)(2,1)} %legendre_ref.1, s32[64]{0:T(128)} %order_in.1, s32[32]{0:T(128)} %start_in.1, s32[32]{0:T(128)} %count_in.1, ...), custom_call_target="tpu_custom_call" | custom-call | tf_op jit(solution)/shard_map/step_terms/pallas_call | solution.py:640
  41.5 3.5 %finish.1 = (bf16[32,8,4,1024]{3,2,1,0:T(4,128)(2,1)}, f32[128,128]{1,0:T(8,128)}) custom-call(f32[128,128]{1,0:T(8,128)S(1)} %get-tuple-element.6.cross_ref, f32[64,128]{1,0:T(8,128)S(1)} %get-tuple-element.7.corner_ref, f32[32,128]{1,0:T(8,128)S(1)} %get-tuple-element.8.ab_ref, bf16[32,8,4,1024]{3,2,1,0:T(4,128)(2,1)S(1)} %get-tuple-element.9.staged_ref), custom_call_target="tpu_custom_call" | custom-call | tf_op jit(solution)/shard_map/finish/pallas_call | solution.py:736

commit v4 on v3

--- a/solution.py
+++ b/solution.py
@@ -42,6 +42,18 @@
         pieces.append(piece)
         x = x - piece.astype(F32)
     return pieces
+
+
+def stacked(x, axis, first):
+    high, middle, low = split(x, 3)
+    order = (high, high, high, middle, middle, low) if first else (high, middle, low, high, middle, high)
+    return jnp.concatenate(order, axis=axis)
+
+
+def fine(a, b, a_axis, b_axis):
+    dims = (((a_axis,), (b_axis,)), ((), ()))
+    a, b = stacked(a, a_axis, True), stacked(b, b_axis, False)
+    return lax.dot_general(a, b, dims, preferred_element_type=F32)
 
 
 def swap(x):
@@ -337,6 +349,35 @@
     def vert_done(kind, source, target):
         over_vert(lambda peer: vert_copy(kind, source, target, vert, peer).wait_send())
 
+    beside = side * half + 1 - place
+    across = (1 - side) * half + place
+    last = (1 - side) * half + 1 - place
+
+    def hand_over(kind, target, slot, key):
+        return pltpu.make_async_remote_copy(
+            src_ref=target.at[slot],
+            dst_ref=target.at[slot],
+            send_sem=vert_send.at[kind, key],
+            recv_sem=vert_recv.at[kind, slot],
+            device_id=(ma, beside),
+            device_id_type=MESH,
+        )
+
+    def gather_start(kind, target):
+        vert_copy(kind, target.at[vert], target, vert, across).start()
+        vert_copy(kind, target.at[vert], target, vert, beside).start()
+
+    def gather_wait(kind, target):
+        vert_copy(kind, target.at[vert], target, across, across).wait_recv()
+        hand_over(kind, target, across, last).start()
+        vert_copy(kind, target.at[vert], target, beside, beside).wait_recv()
+        vert_copy(kind, target.at[vert], target, last, last).wait_recv()
+
+    def gather_done(kind, target):
+        vert_copy(kind, target.at[vert], target, vert, across).wait_send()
+        vert_copy(kind, target.at[vert], target, vert, beside).wait_send()
+        hand_over(kind, target, across, last).wait_send()
+
     ma_start(0, message, gathered)
     gathered[ma] = message[...]
 
@@ -431,7 +472,7 @@
     back_x = turned[3 * vectors :]
     packed[vert, :, : 2 * terms] = g_x
     packed[vert, :, 2 * terms :] = g_y
-    vert_start(0, packed.at[vert], packed)
+    gather_start(0, packed)
     send_far(cuts[0], cuts[1])
 
     signs = sign.astype(BF16)
@@ -445,7 +486,7 @@
         lhs[at, : 2 * terms] = piece_x
         lhs[at, 2 * terms :] = piece_y
 
-    vert_wait(0, packed.at[vert], packed)
+    gather_wait(0, packed)
     everyone = packed[...].reshape(total, 4 * terms)
     found = mm_nt(lhs[...], everyone)
     found = [found[n * vectors : (n + 1) * vectors] for n in range(6)]
@@ -480,7 +521,7 @@
 
     ma_wait(1, row_a, land_a)
     sum_a[vert] = jnp.sum(land_a[...], axis=0)
-    vert_start(1, sum_a.at[vert], sum_a)
+    gather_start(1, sum_a)
     send_far(cuts[1], cuts[2])
     ma_start(2, row_b, land_b)
     ma_wait(4, row_e, land_e)
@@ -488,7 +529,7 @@
     vert_start(4, sum_e.at[vert], sum_e)
     send_far(cuts[2], pieces)
 
-    vert_wait(1, sum_a.at[vert], sum_a)
+    gather_wait(1, sum_a)
     inverse_count = 1.0 / (n_ma * orders * parts * degrees)
     work[:, :total] = sum_a[...].reshape(total, total) * inverse_count
     work[:, total:] = (iota((total, total), 0) == iota((total, total), 1)).astype(F32)
@@ -612,10 +653,10 @@
 
     lax.fori_loop(0, pieces, far_done, 0)
     ma_done(0, message, gathered)
-    vert_done(0, packed.at[vert], packed)
+    gather_done(0, packed)
     ma_done(1, row_a, land_a)
     ma_done(2, row_b, land_b)
-    vert_done(1, sum_a.at[vert], sum_a)
+    gather_done(1, sum_a)
     vert_done(2, sum_b.at[vert], sum_b)
     ma_done(4, row_e, land_e)
     vert_done(4, sum_e.at[vert], sum_e)
@@ -710,12 +751,13 @@
     ab = jnp.concatenate([ab[:, :size], ab[:, size:]], axis=0)
     inverse, diagonal = corner_ref[:, :size], corner_ref[:, size:]
     beside = jnp.dot(inverse, ab, precision=HIGHEST, preferred_element_type=F32)
-    taken = lax.dot_general(
-        beside, beside, (((0,), (0,)), ((), ())), precision=HIGHEST, preferred_element_type=F32
-    )
+    taken = fine(beside, beside, 0, 0)
     unit = (iota((size, size), 0) == iota((size, size), 1)).astype(F32)
     work[:, :total] = jnp.concatenate([diagonal - taken, jnp.zeros_like(unit)], axis=1)
-    work[:, total:] = jnp.concatenate([-beside.T, unit], axis=1)
+    turned = lax.dot_general(
+        ab, inverse, (((0,), (1,)), ((), ())), precision=HIGHEST, preferred_element_type=F32
+    )
+    work[:, total:] = jnp.concatenate([-turned, unit], axis=1)
 
     def step(p, carry):
         factor_panel(work, p)
@@ -724,10 +766,7 @@
     lax.fori_loop(0, size // PANEL, step, 0)
     upper = (iota((size, total), 0) == iota((size, total), 1)).astype(F32)
     outer = jnp.concatenate([upper, work[:, total:]], axis=0)
-    crossed = jnp.dot(outer, cross_ref[...], precision=HIGHEST, preferred_element_type=F32)
-    ritz_ref[...] = lax.dot_general(
-        crossed, outer, NT, precision=HIGHEST, preferred_element_type=F32
-    )
+    ritz_ref[...] = fine(fine(outer, cross_ref[...], 1, 0), outer, 1, 1)
     out.wait()
 
 

time: 45.1 us -> 44.7 us (level)
  no operation moved by 1% of the time
where the time goes in v4:
time: 44.7 us; the launch traced here: 44.6 us
  Pallas kernels  44 us (98%)
  between operations  0.64 us (1%)
    pallas_call x1, Pallas kernels, step_terms(): pl.pallas_call(functools.partial(step_kernel, n_ma, n_vert, live), out_sh...  40.6 us
    pallas_call x1, Pallas kernels, finish(): pl.pallas_call(finish_kernel, out_shape=(jax.ShapeDtypeStruct(staged.shap...  3.38 us

profile of v4, /device:TPU:0, one launch (start us, length us, event | category | flops | bytes accessed | tf_op | source)
XLA Modules:
  0.0 44.6 jit_solution(14334711851296162479)
XLA Ops:
  0.6 40.6 %step_terms.1 = (f32[128,128]{1,0:T(8,128)S(1)}, f32[64,128]{1,0:T(8,128)S(1)}, f32[32,128]{1,0:T(8,128)S(1)}, bf16[32,8,4,1024]{3,2,1,0:T(4,128)(2,1)S(1)}) custom-call(bf16[32,8,32,128]{3,2,1,0:T(8,128)(2,1)} %bitcast.5, bf16[8,2,32,1024]{3,2,1,0:T(8,128)(2,1)} %legendre_ref.1, s32[64]{0:T(128)} %order_in.1, s32[32]{0:T(128)} %start_in.1, s32[32]{0:T(128)} %count_in.1, ...), custom_call_target="tpu_custom_call" | custom-call | tf_op jit(solution)/shard_map/step_terms/pallas_call | solution.py:681
  41.2 3.4 %finish.1 = (bf16[32,8,4,1024]{3,2,1,0:T(4,128)(2,1)}, f32[128,128]{1,0:T(8,128)}) custom-call(f32[128,128]{1,0:T(8,128)S(1)} %get-tuple-element.6.cross_ref, f32[64,128]{1,0:T(8,128)S(1)} %get-tuple-element.7.corner_ref, f32[32,128]{1,0:T(8,128)S(1)} %get-tuple-element.8.ab_ref, bf16[32,8,4,1024]{3,2,1,0:T(4,128)(2,1)S(1)} %get-tuple-element.9.staged_ref), custom_call_target="tpu_custom_call" | custom-call | tf_op jit(solution)/shard_map/finish/pallas_call | solution.py:775
